TPU v7x, 32 devices: a whole 2x2x4 slice. The times are simulated.
32 devices in a mesh: replica: 8 (over z, y), tensor: 4 (over x, core).
Axes of the slice: x: 2, y: 2, z: 4, core: 2. Of those that a mesh axis runs over, the one named last changes fastest.
Arguments:
- base_stream: bfloat16 [32, 8192], P('tensor', 'replica'), may hold values from -6 to 6
- out_weight: bfloat16 [64, 128, 8192], P('tensor', 'replica'), may hold values from -0.5 to 0.5
- queries: bfloat16 [4, 32, 64, 128], P(None, 'replica', 'tensor'), may hold values from -5 to 5
- cache_keys: bfloat16 [32, 8, 1536, 128], P('replica', 'tensor'), may hold values from -5 to 5
- cache_values: bfloat16 [32, 8, 1536, 128], P('replica', 'tensor'), may hold values from -6 to 6
- new_keys: bfloat16 [4, 32, 8, 128], P(None, 'replica', 'tensor'), may hold values from -5 to 5
- new_values: bfloat16 [4, 32, 8, 128], P(None, 'replica', 'tensor'), may hold values from -6 to 6
- lengths: int32 [32], P('replica'), may hold values from 384 to 1536
- finished: int32 [32], replicated, may hold values 0 or 1
- owners: int32 [32, 1], replicated, may hold values from 0 to 7; in each aligned block of 32 rows (0 to 31, 32 to 63, ...) at most 4 rows name the same one
Outputs:
- updates: bfloat16 [4, 32, 8192], P(None, 'tensor', 'replica')
- trainer_rows: bfloat16 [8, 4, 8192], P('replica', 'tensor')
Inputs may be any that keep to these rules, and one draw needn't show every extreme that they name: `owners`: no owner is named by more than 4 rows, and one owner is named by exactly 4.
All inputs are finite; a program needn't handle non-finite values.
Results may differ from a plain program's by a relative error of at most 0.013.
Values may be sent and summed in bfloat16 or wider, within the bound.
No kernel may reach another device: no remote copies, remote signals or barrier semaphores. Data moves between devices by JAX's collectives and lax.ppermute only.
A program may use at most 128 MiB of HBM per device.

v0:
```python
import math
import jax
import jax.numpy as jnp
from jax import lax
from jax.sharding import PartitionSpec as P

SLOT_DEV = 1


def attend(queries, cache_keys, cache_values, new_keys, new_values, lengths):
    steps_count, row_count, heads_here, head_size = queries.shape
    kv_here = cache_keys.shape[1]
    positions_count = cache_keys.shape[2]
    group_size = heads_here // kv_here
    score_scale = 1.0 / math.sqrt(head_size)
    grouped = queries.reshape(steps_count, row_count, kv_here, group_size, head_size)
    cache_scores = (
        jnp.einsum("tbgqd,bgcd->tbgqc", grouped, cache_keys, preferred_element_type=jnp.float32)
        * score_scale
    )
    positions = lax.broadcasted_iota(jnp.int32, (1, row_count, 1, 1, positions_count), 4)
    is_valid = positions < lengths[None, :, None, None, None]
    cache_scores = jnp.where(is_valid, cache_scores, jnp.float32(-1e30))
    fresh_scores = (
        jnp.einsum("tbgqd,ubgd->tbgqu", grouped, new_keys, preferred_element_type=jnp.float32)
        * score_scale
    )
    step_now = lax.broadcasted_iota(jnp.int32, (steps_count, 1, 1, 1, steps_count), 0)
    step_then = lax.broadcasted_iota(jnp.int32, (steps_count, 1, 1, 1, steps_count), 4)
    fresh_scores = jnp.where(step_then <= step_now, fresh_scores, jnp.float32(-1e30))
    highest = jnp.maximum(
        jnp.max(cache_scores, axis=-1, keepdims=True), jnp.max(fresh_scores, axis=-1, keepdims=True)
    )
    cache_weights = jnp.exp(cache_scores - highest)
    fresh_weights = jnp.exp(fresh_scores - highest)
    totals = jnp.sum(cache_weights, axis=-1, keepdims=True) + jnp.sum(
        fresh_weights, axis=-1, keepdims=True
    )
    cache_probs = (cache_weights / totals).astype(jnp.bfloat16)
    fresh_probs = (fresh_weights / totals).astype(jnp.bfloat16)
    mixed = jnp.einsum(
        "tbgqc,bgcd->tbgqd", cache_probs, cache_values, preferred_element_type=jnp.float32
    )
    mixed = mixed + jnp.einsum(
        "tbgqu,ubgd->tbgqd", fresh_probs, new_values, preferred_element_type=jnp.float32
    )
    return mixed.reshape(steps_count, row_count, heads_here * head_size).astype(jnp.bfloat16)


def reduce_heads(partial_value):
    rounded = partial_value.astype(jnp.bfloat16)
    totals = lax.psum(rounded, "tensor").astype(jnp.float32)
    share = totals.shape[1] // lax.axis_size("tensor")
    return lax.dynamic_slice_in_dim(totals, lax.axis_index("tensor") * share, share, 1)


def shards(
    base_stream,
    out_weight,
    queries,
    cache_keys,
    cache_values,
    new_keys,
    new_values,
    lengths,
    finished,
    owners,
):
    heads_here = out_weight.shape[0]
    regrouped = lax.all_to_all(out_weight, "replica", split_axis=2, concat_axis=1, tiled=True)
    weight_local = regrouped.reshape(heads_here * regrouped.shape[1], regrouped.shape[2])
    attended = attend(queries, cache_keys, cache_values, new_keys, new_values, lengths)
    partial_value = jnp.einsum(
        "tbf,fc->tbc",
        lax.all_gather(attended, "replica", axis=1, tiled=True),
        weight_local,
        preferred_element_type=jnp.float32,
    )
    summed = reduce_heads(partial_value)
    updates = summed.astype(jnp.bfloat16)
    stream = base_stream.astype(jnp.float32) + jnp.sum(updates.astype(jnp.float32), axis=0)
    stream_rounded = stream.astype(jnp.bfloat16)
    all_streams = lax.all_gather(stream_rounded, "tensor", axis=0, tiled=True)
    owner_count = lax.axis_size("replica")
    owner_ids = lax.broadcasted_iota(jnp.int32, (1, owner_count), 1)
    onehot = (owners == owner_ids).astype(jnp.int32)
    before = jnp.cumsum(onehot, axis=0) - onehot
    slot_rank = jnp.sum(before * onehot, axis=1)
    first_slot = lax.axis_index("tensor") * SLOT_DEV
    slot_ids = first_slot + lax.broadcasted_iota(jnp.int32, (1, 1, SLOT_DEV), 2)
    chosen = (
        onehot[:, :, None]
        * (slot_rank[:, None, None] == slot_ids).astype(jnp.int32)
        * finished[:, None, None]
    )
    selector = chosen.astype(jnp.bfloat16)
    outgoing = jnp.einsum(
        "jos,jc->osc", selector, all_streams, preferred_element_type=jnp.float32
    ).astype(jnp.bfloat16)
    trainer_rows = lax.all_to_all(outgoing, "replica", split_axis=0, concat_axis=2, tiled=True)
    return (updates, trainer_rows)


def solution(mesh):
    placed = (
        P("tensor", "replica"),
        P("tensor", "replica", None),
        P(None, "replica", "tensor", None),
        P("replica", "tensor", None, None),
        P("replica", "tensor", None, None),
        P(None, "replica", "tensor", None),
        P(None, "replica", "tensor", None),
        P("replica"),
        P(),
        P(),
    )
    return jax.shard_map(
        shards,
        mesh=mesh,
        in_specs=placed,
        out_specs=(P(None, "tensor", "replica"), P("replica", "tensor", None)),
        check_vma=False,
    )
```

profile of v0, /device:TPU:0, one launch (start us, length us, event | category | flops | bytes accessed | tf_op | source)
XLA Modules:
  0.0 318.9 jit_solution(999825138677871653)
XLA Ops:
  7.2 27.8 %copy.29 = bf16[16,16,8192]{1,0,2:T(8,128)(2,1)} copy(bf16[16,16,8192]{2,1,0:T(8,128)(2,1)} %param.11) | data formatting | bytes 8388608 | tf_op args[1]
  35.0 37.7 %reshape.116 = bf16[8,2,131072]{2,1,0:T(2,128)(2,1)} reshape(bf16[8192,16,16]{2,1,0:T(8,128)(2,1)} %bitcast.60) | data formatting | bytes 8388608
  72.7 7.4 %all-to-all-start = ((bf16[8,2,131072]{2,1,0:T(2,128)(2,1)}), bf16[8,2,131072]{2,1,0:T(2,128)(2,1)}, u32[]{:S(2)}, u32[]{:S(2)}) async-start(bf16[8,2,131072]{2,1,0:T(2,128)(2,1)} %reshape.116), calls=%async_computation | async-start | bytes 8388608 | tf_op jit(solution)/shard_map/all_to_all | solution.py:70
  80.2 0.4 fusion.44
  80.7 0.1 iota_compare_fusion
  80.8 1.2 fusion.43
  82.0 0.1 fusion.31
  82.1 0.4 fusion.13
  82.5 0.2 fusion.32
  82.7 0.7 fusion.20
  83.5 0.1 fusion.35
  83.6 0.2 select_reduce_fusion
  83.8 112.7 %all_gather.6 = bf16[4,32,2048]{2,0,1:T(4,128)(2,1)} all-gather(bf16[4,4,2048]{2,0,1:T(4,128)(2,1)S(1)} %reshape.115), channel_id=1, replica_groups=mesh['replica'=8,'tensor'=4] {'replica'}, dimensions={1}, use_global_device_ids=true | all-gather | bytes 589824 | tf_op jit(solution)/shard_map/all_gather | solution.py:75
  196.5 25.8 %reshape.117 = bf16[8192,16,16]{2,1,0:T(8,128)(2,1)} reshape(bf16[8,2,131072]{2,1,0:T(2,128)(2,1)} %all-to-all-done) | data formatting | bytes 8388608
  222.3 32.9 %copy.30 = bf16[16,16,8,1024]{3,1,2,0:T(8,128)(2,1)} copy(bf16[16,16,8,1024]{1,0,3,2:T(8,128)(2,1)} %bitcast.59) | data formatting | bytes 8388608 | tf_op jit(solution)/shard_map/all_to_all | solution.py:70
  255.2 4.2 %convolution_convert_fusion = bf16[4,32,1024]{2,1,0:T(8,128)(2,1)} fusion(bf16[2048,1024,1]{1,0,2:T(8,128)(2,1)} %bitcast.61, bf16[4,32,2048]{2,0,1:T(4,128)(2,1)} %all_gather.6), kind=kOutput, calls=%fused_computation.10 | convolution fusion | flops 537001984 | bytes 4980736 | tf_op jit(solution)/shard_map/tbf,fc->tbc/dot_general | solution.py:73
  259.5 31.9 %all-reduce.2.cloned.1.call-done = bf16[4,32,1024]{2,1,0:T(8,128)(2,1)} async-done(((bf16[4,32,1024]{2,1,0:T(8,128)(2,1)}), bf16[4,32,1024]{2,1,0:T(8,128)(2,1)}) %all-reduce.2.cloned.1.call-update) | async-done | bytes 262160 | tf_op jit(solution)/shard_map/psum | solution.py:52
  291.3 1.5 convert_reduce_fusion
  292.8 5.2 %all_gather.7 = bf16[32,1024]{1,0:T(8,128)(2,1)S(1)} all-gather(bf16[8,1024]{1,0:T(8,128)(2,1)S(1)} %add_convert_fusion), channel_id=1, replica_groups=mesh['replica'=8,'tensor'=4] {'tensor'}, dimensions={0}, use_global_device_ids=true | all-gather | bytes 81920 | tf_op jit(solution)/shard_map/all_gather | solution.py:83
  298.1 0.3 fusion.25
  298.3 0.5 broadcast.58
  298.9 0.7 reduce
  299.5 11.9 %all_to_all.27 = bf16[8,2,512]{2,1,0:T(2,128)(2,1)S(1)} all-to-all(bf16[8,2,512]{2,1,0:T(2,128)(2,1)S(1)} %reshape.118), channel_id=1, replica_groups=mesh['replica'=8,'tensor'=4] {'replica'}, dimensions={0} | all-to-all | bytes 32768 | tf_op jit(solution)/shard_map/all_to_all | solution.py:100
  311.4 0.6 reshape.119
  (32 shorter events, 0.2 us)
Async XLA Ops:
  7.2 73.6 %copy-start = (bf16[4,2,1536,128]{3,2,1,0:T(8,128)(2,1)S(1)}, bf16[4,2,1536,128]{3,2,1,0:T(8,128)(2,1)}, u32[]{:S(2)}) copy-start(bf16[4,2,1536,128]{3,2,1,0:T(8,128)(2,1)} %param.13) | copy-start | bytes 9437188
  72.7 7.5 %copy-start.2 = (bf16[4,4,16,128]{3,2,1,0:T(8,128)(2,1)S(1)}, bf16[4,4,16,128]{3,2,1,0:T(8,128)(2,1)}, u32[]{:S(2)}) copy-start(bf16[4,4,16,128]{3,2,1,0:T(8,128)(2,1)} %param.12) | copy-start | bytes 196612
  72.7 7.5 %copy-start.7 = (bf16[4,4,2,128]{3,2,1,0:T(2,128)(2,1)S(1)}, bf16[4,4,2,128]{3,2,1,0:T(2,128)(2,1)}, u32[]{:S(2)}) copy-start(bf16[4,4,2,128]{3,2,1,0:T(2,128)(2,1)} %param.15) | copy-start | bytes 24580
  72.7 8.0 %copy-start.5 = (s32[4]{0:T(128)S(1)}, s32[4]{0:T(128)}, u32[]{:S(2)}) copy-start(s32[4]{0:T(128)} %param.17) | copy-start | bytes 52
  72.7 123.8 %all-to-all-start = ((bf16[8,2,131072]{2,1,0:T(2,128)(2,1)}), bf16[8,2,131072]{2,1,0:T(2,128)(2,1)}, u32[]{:S(2)}, u32[]{:S(2)}) async-start(bf16[8,2,131072]{2,1,0:T(2,128)(2,1)} %reshape.116), calls=%async_computation | async-start | bytes 8388608 | tf_op jit(solution)/shard_map/all_to_all | solution.py:70
  80.2 211.2 %all-reduce.2.cloned.1.call-start = ((), (), s32[]{:S(2)}) async-start(), calls=%async_computation.2 | async-start | bytes 524288 | tf_op jit(solution)/shard_map/psum | solution.py:52
  80.8 1.7 copy-start.8
  80.8 1.9 copy-start.6
  82.7 0.8 copy-start.4
  255.2 56.9 %copy-start.1 = (bf16[4,2,1536,128]{3,2,1,0:T(8,128)(2,1)S(1)}, bf16[4,2,1536,128]{3,2,1,0:T(8,128)(2,1)}, u32[]{:S(2)}) copy-start(bf16[4,2,1536,128]{3,2,1,0:T(8,128)(2,1)} %param.13) | copy-start | bytes 9437188
  255.2 37.6 %copy-start.3 = (bf16[8,1024]{1,0:T(8,128)(2,1)S(1)}, bf16[8,1024]{1,0:T(8,128)(2,1)}, u32[]{:S(2)}) copy-start(bf16[8,1024]{1,0:T(8,128)(2,1)} %param.10) | copy-start | bytes 49156
  255.2 42.9 %copy-start.9 = (s32[32]{0:T(128)S(1)}, s32[32]{0:T(128)}, u32[]{:S(2)}) copy-start(s32[32]{0:T(128)} %param.18) | copy-start | bytes 388
Sparse Core Ops, SparseCore 0:
  259.6 31.7 all-reduce.1
where the time goes:
time: 321 us; the launch traced here: 319 us
  blocking collectives  130 us (40%)
  local copies, waits for them, and re-layouts  125 us (39%)
  waiting for transfers between devices  31.9 us (10%)
  between operations  14.2 us (4%)
  starting transfers between devices  7.48 us (2%)
  matrix products  7.07 us (2%)
    all_gather x1, blocking collectives, shards(): lax.all_gather(attended, 'replica', axis=1, tiled=True)  113 us
    unnamed x25, local copies, waits for them, and re-layouts  92 us
    all_to_all x1, local copies, waits for them, and re-layouts, shards(): lax.all_to_all(out_weight, 'replica', split_axis=2, concat_axis=1, tiled=...  32.9 us
    psum x1, waiting for transfers between devices, reduce_heads(): totals = lax.psum(rounded, 'tensor').astype(jnp.float32)  31.9 us
    all_to_all x1, blocking collectives, shards(): lax.all_to_all(outgoing, 'replica', split_axis=0, concat_axis=2, tiled=True)  11.9 us
    all_to_all x1, starting transfers between devices, shards(): lax.all_to_all(out_weight, 'replica', split_axis=2, concat_axis=1, tiled=...  7.45 us
  transfers between devices with their start and end apart: 2, of which 1 were waited for; matrix products, arithmetic and copies ran while one was open for 1% of the time, Pallas kernels for 0%

commit v1 on v0

--- a/solution.py
+++ b/solution.py
@@ -5,6 +5,11 @@
 from jax.sharding import PartitionSpec as P
 
 SLOT_DEV = 1
+
+
+def convert_views(matrix, named_axis):
+    block_out = jnp.sum(jax.lax.all_gather(matrix, named_axis), 0)
+    return block_out
 
 
 def attend(queries, cache_keys, cache_values, new_keys, new_values, lengths):
@@ -49,7 +54,7 @@
 
 def reduce_heads(partial_value):
     rounded = partial_value.astype(jnp.bfloat16)
-    totals = lax.psum(rounded, "tensor").astype(jnp.float32)
+    totals = convert_views(rounded, "tensor").astype(jnp.float32)
     share = totals.shape[1] // lax.axis_size("tensor")
     return lax.dynamic_slice_in_dim(totals, lax.axis_index("tensor") * share, share, 1)
 

time: 321 us -> 306 us (0.953)
  waiting for transfers between devices: 31.9 us -> 16 us
    psum x1 -> x0, waiting for transfers between devices: 31.9 us -> none  [reduce_heads(): totals = lax.psum(rounded, 'tensor').astype(jnp.float32)]
    all_gather x0 -> x1, waiting for transfers between devices: none -> 16 us  [convert_views(): block_out = jnp.sum(jax.lax.all_gather(matrix, named_axis), 0)]
where the time goes in v1:
time: 306 us; the launch traced here: 304 us
  blocking collectives  130 us (42%)
  local copies, waits for them, and re-layouts  125 us (41%)
  waiting for transfers between devices  16 us (5%)
  between operations  14.2 us (5%)
  starting transfers between devices  7.49 us (2%)
  matrix products  7.08 us (2%)
  other arithmetic  3.59 us (1%)
    all_gather x1, blocking collectives, shards(): lax.all_gather(attended, 'replica', axis=1, tiled=True)  113 us
    unnamed x25, local copies, waits for them, and re-layouts  92 us
    all_to_all x1, local copies, waits for them, and re-layouts, shards(): lax.all_to_all(out_weight, 'replica', split_axis=2, concat_axis=1, tiled=...  32.9 us
    all_gather x1, waiting for transfers between devices, convert_views(): block_out = jnp.sum(jax.lax.all_gather(matrix, named_axis), 0)  16 us
    all_to_all x1, blocking collectives, shards(): lax.all_to_all(outgoing, 'replica', split_axis=0, concat_axis=2, tiled=True)  11.9 us
    all_to_all x1, starting transfers between devices, shards(): lax.all_to_all(out_weight, 'replica', split_axis=2, concat_axis=1, tiled=...  7.45 us
  transfers between devices with their start and end apart: 2, of which 1 were waited for; matrix products, arithmetic and copies ran while one was open for 1% of the time, Pallas kernels for 0%

profile of v1, /device:TPU:0, one launch (start us, length us, event | category | flops | bytes accessed | tf_op | source)
XLA Modules:
  0.0 303.9 jit_solution(15393141523697731162)
XLA Ops:
  7.2 27.8 %copy.29 = bf16[16,16,8192]{1,0,2:T(8,128)(2,1)} copy(bf16[16,16,8192]{2,1,0:T(8,128)(2,1)} %param.11) | data formatting | bytes 8388608 | tf_op args[1]
  35.0 37.7 %reshape.117 = bf16[8,2,131072]{2,1,0:T(2,128)(2,1)} reshape(bf16[8192,16,16]{2,1,0:T(8,128)(2,1)} %bitcast.61) | data formatting | bytes 8388608
  72.7 7.4 %all-to-all-start = ((bf16[8,2,131072]{2,1,0:T(2,128)(2,1)}), bf16[8,2,131072]{2,1,0:T(2,128)(2,1)}, u32[]{:S(2)}, u32[]{:S(2)}) async-start(bf16[8,2,131072]{2,1,0:T(2,128)(2,1)} %reshape.117), calls=%async_computation | async-start | bytes 8388608 | tf_op jit(solution)/shard_map/all_to_all | solution.py:75
  80.2 0.4 fusion.44
  80.7 0.1 iota_compare_fusion
  80.8 1.2 fusion.43
  82.0 0.1 fusion.31
  82.1 0.4 fusion.13
  82.5 0.2 fusion.32
  82.7 0.7 fusion.20
  83.5 113.1 %all_gather.12 = bf16[4,32,2048]{2,0,1:T(4,128)(2,1)} all-gather(bf16[4,4,2048]{2,0,1:T(4,128)(2,1)S(1)} %reshape.116), channel_id=1, replica_groups=mesh['replica'=8,'tensor'=4] {'replica'}, dimensions={1}, use_global_device_ids=true | all-gather | bytes 589824 | tf_op jit(solution)/shard_map/all_gather | solution.py:80
  196.5 25.8 %reshape.118 = bf16[8192,16,16]{2,1,0:T(8,128)(2,1)} reshape(bf16[8,2,131072]{2,1,0:T(2,128)(2,1)} %all-to-all-done) | data formatting | bytes 8388608
  222.3 32.9 %copy.30 = bf16[16,16,8,1024]{3,1,2,0:T(8,128)(2,1)} copy(bf16[16,16,8,1024]{1,0,3,2:T(8,128)(2,1)} %bitcast.60) | data formatting | bytes 8388608 | tf_op jit(solution)/shard_map/all_to_all | solution.py:75
  255.2 4.2 %convolution_convert_fusion = bf16[4,32,1024]{2,1,0:T(8,128)(2,1)} fusion(bf16[2048,1024,1]{1,0,2:T(8,128)(2,1)} %bitcast.62, bf16[4,32,2048]{2,0,1:T(4,128)(2,1)} %all_gather.12), kind=kOutput, calls=%fused_computation.10 | convolution fusion | flops 537001984 | bytes 4980736 | tf_op jit(solution)/shard_map/tbf,fc->tbc/dot_general | solution.py:78
  259.6 0.2 select_reduce_fusion
  259.8 16.0 %all-gather.3.cloned.1.call-done = bf16[16,32,1024]{2,1,0:T(8,128)(2,1)} async-done(((bf16[4,32,1024]{2,1,0:T(8,128)(2,1)}), bf16[16,32,1024]{2,1,0:T(8,128)(2,1)}) %all-gather.3.cloned.1.call-update) | async-done | bytes 1048592 | tf_op jit(solution)/shard_map/all_gather | solution.py:11
  275.8 1.4 reduce_sum.50
  277.2 0.6 convert_reduce_fusion
  277.9 5.2 %all_gather.15 = bf16[32,1024]{1,0:T(8,128)(2,1)S(1)} all-gather(bf16[8,1024]{1,0:T(8,128)(2,1)S(1)} %add_convert_fusion), channel_id=1, replica_groups=mesh['replica'=8,'tensor'=4] {'tensor'}, dimensions={0}, use_global_device_ids=true | all-gather | bytes 81920 | tf_op jit(solution)/shard_map/all_gather | solution.py:88
  283.1 0.3 fusion.25
  283.4 0.5 broadcast.58
  283.9 0.7 reduce.1
  284.6 11.9 %all_to_all.27 = bf16[8,2,512]{2,1,0:T(2,128)(2,1)S(1)} all-to-all(bf16[8,2,512]{2,1,0:T(2,128)(2,1)S(1)} %reshape.119), channel_id=1, replica_groups=mesh['replica'=8,'tensor'=4] {'replica'}, dimensions={0} | all-to-all | bytes 32768 | tf_op jit(solution)/shard_map/all_to_all | solution.py:105
  296.5 0.6 reshape.120
  (33 shorter events, 0.3 us)
Async XLA Ops:
  7.2 73.6 %copy-start = (bf16[4,2,1536,128]{3,2,1,0:T(8,128)(2,1)S(1)}, bf16[4,2,1536,128]{3,2,1,0:T(8,128)(2,1)}, u32[]{:S(2)}) copy-start(bf16[4,2,1536,128]{3,2,1,0:T(8,128)(2,1)} %param.13) | copy-start | bytes 9437188
  72.7 7.5 %copy-start.2 = (bf16[4,4,16,128]{3,2,1,0:T(8,128)(2,1)S(1)}, bf16[4,4,16,128]{3,2,1,0:T(8,128)(2,1)}, u32[]{:S(2)}) copy-start(bf16[4,4,16,128]{3,2,1,0:T(8,128)(2,1)} %param.12) | copy-start | bytes 196612
  72.7 7.5 %copy-start.7 = (bf16[4,4,2,128]{3,2,1,0:T(2,128)(2,1)S(1)}, bf16[4,4,2,128]{3,2,1,0:T(2,128)(2,1)}, u32[]{:S(2)}) copy-start(bf16[4,4,2,128]{3,2,1,0:T(2,128)(2,1)} %param.15) | copy-start | bytes 24580
  72.7 8.0 %copy-start.5 = (s32[4]{0:T(128)S(1)}, s32[4]{0:T(128)}, u32[]{:S(2)}) copy-start(s32[4]{0:T(128)} %param.17) | copy-start | bytes 52
  72.7 123.8 %all-to-all-start = ((bf16[8,2,131072]{2,1,0:T(2,128)(2,1)}), bf16[8,2,131072]{2,1,0:T(2,128)(2,1)}, u32[]{:S(2)}, u32[]{:S(2)}) async-start(bf16[8,2,131072]{2,1,0:T(2,128)(2,1)} %reshape.117), calls=%async_computation | async-start | bytes 8388608 | tf_op jit(solution)/shard_map/all_to_all | solution.py:75
  80.2 195.6 %all-gather.3.cloned.1.call-start = ((), (), s32[]{:S(2)}) async-start(), calls=%async_computation.2 | async-start | bytes 1310720 | tf_op jit(solution)/shard_map/all_gather | solution.py:11
  80.8 1.7 copy-start.8
  80.8 1.9 copy-start.6
  255.2 41.9 %copy-start.1 = (bf16[4,2,1536,128]{3,2,1,0:T(8,128)(2,1)S(1)}, bf16[4,2,1536,128]{3,2,1,0:T(8,128)(2,1)}, u32[]{:S(2)}) copy-start(bf16[4,2,1536,128]{3,2,1,0:T(8,128)(2,1)} %param.13) | copy-start | bytes 9437188
  255.2 4.3 %copy-start.4 = (s32[32,1]{0,1:T(1,128)S(1)}, s32[32,1]{0,1:T(1,128)}, u32[]{:S(2)}) copy-start(s32[32,1]{0,1:T(1,128)} %param.19) | copy-start | bytes 388
  255.2 22.7 %copy-start.3 = (bf16[8,1024]{1,0:T(8,128)(2,1)S(1)}, bf16[8,1024]{1,0:T(8,128)(2,1)}, u32[]{:S(2)}) copy-start(bf16[8,1024]{1,0:T(8,128)(2,1)} %param.10) | copy-start | bytes 49156
  255.2 27.9 %copy-start.9 = (s32[32]{0:T(128)S(1)}, s32[32]{0:T(128)}, u32[]{:S(2)}) copy-start(s32[32]{0:T(128)} %param.18) | copy-start | bytes 388
Sparse Core Ops, SparseCore 0:
  259.6 16.1 all-gather.2
